TPU v7x, 32 devices: a whole 2x2x4 slice. The times are simulated.
32 devices in a mesh: grp: 4 (over y, x), slab: 8 (over z, core).
Axes of the slice: x: 2, y: 2, z: 4, core: 2. Of those that a mesh axis runs over, the one named last changes fastest.
Arguments:
- velocity: float32 [16, 3, 4, 16384], P(None, None, 'grp', 'slab'), may hold values from -6 to 6
- old_basis: bfloat16 [64, 3, 4, 16384], P(None, None, None, 'slab'), may hold values from -6 to 6
- singular_values: float32 [64], replicated, may hold values from 0.7 to 1.4
- thickness: int32 [4, 8], P('grp', 'slab'), may hold values from 1 to 4, as said below
Outputs:
- gram_matrix: float32 [80, 80], replicated
- new_basis: bfloat16 [64, 3, 4, 16384], P(None, None, None, 'slab')
- offsets: int32 [4, 8], P('grp', 'slab')
Inputs may be any that keep to these rules, and one draw needn't show every extreme that they name: `thickness`: the entry at row-major position p differs from 1 + (p * 3) // 32 by at most one. The first entry is 1 and the last is 4.
All inputs are finite; a program needn't handle non-finite values.
Results may differ from a plain program's by a relative error of at most 0.0004.
The roundings to bfloat16 on the way count: a program that leaves them out, or rounds other values in their place, can miss the bound.
Values may be sent and summed in bfloat16 or wider, within the bound.
A program may use at most 64 MiB of HBM per device.

v0:
```python
import jax
import jax.numpy as jnp
from jax import lax
from jax.sharding import PartitionSpec as P

PLANE = 512


def entering(value, axis, join, neutral):
    count, mine = (lax.axis_size(axis), lax.axis_index(axis))
    pieces = lax.all_gather(value, axis)
    total = jnp.full_like(value, 0) + jnp.asarray(neutral, value.dtype)

    def step(position, total):
        longer = join(total, pieces[position])
        return jnp.where(position < mine, longer, total)

    return lax.fori_loop(0, count - 1, step, total)


def orthonormalize(matrix, rank_count):
    iterate = matrix * (0.5 * rank_count**0.5 / jnp.sqrt(jnp.sum(matrix * matrix)))
    for sweep_index in range(4):
        product = jnp.dot(iterate.T, iterate, precision=lax.Precision.HIGHEST)
        iterate = 1.5 * iterate - 0.5 * jnp.dot(iterate, product, precision=lax.Precision.HIGHEST)
    return iterate


def add_counts(earlier, later):
    return earlier + later


def per_device(velocity, old_basis, singular_values, thickness):
    capacity = velocity.shape[-1]
    snap_count = velocity.shape[0]
    rank_count = old_basis.shape[0]
    plane_ids = lax.broadcasted_iota(jnp.int32, (1, capacity), 1) // PLANE
    own_mask = plane_ids < thickness
    masked = jnp.where(
        own_mask[None, None], velocity.astype(jnp.bfloat16), jnp.zeros((), jnp.bfloat16)
    )
    live_cells = lax.psum(jnp.sum(thickness).astype(jnp.float32) * PLANE, ("grp", "slab"))
    region_index = lax.axis_index("grp")
    own_basis = lax.dynamic_slice_in_dim(old_basis, region_index, 1, 2)
    columns = jnp.where(own_mask[None, None], own_basis, jnp.zeros((), jnp.bfloat16))
    stacked = jnp.concatenate([columns.reshape(rank_count, -1), masked.reshape(snap_count, -1)], 0)
    raw_gram = lax.dot_general(
        stacked, stacked, (((1,), (1,)), ((), ())), preferred_element_type=jnp.float32
    )
    partial_terms = (raw_gram,)
    summed = lax.psum((partial_terms[0],), ("grp", "slab"))
    scales = jnp.concatenate([singular_values, jnp.ones((snap_count,), jnp.float32)])
    gram_matrix = summed[0] * scales[:, None] * scales[None, :] / (3.0 * live_cells)
    mixing = orthonormalize(gram_matrix[:, :rank_count], rank_count)
    mixing_rows = (mixing * scales[:, None]).T.astype(jnp.bfloat16)
    updated = jnp.dot(mixing_rows, stacked, preferred_element_type=jnp.float32).astype(jnp.bfloat16)
    new_basis = lax.all_gather(
        updated.reshape(rank_count, 3, 1, capacity), "grp", axis=2, tiled=True
    )
    offsets = entering(thickness, ("grp", "slab"), add_counts, jnp.zeros_like(thickness))
    return (gram_matrix, new_basis, offsets)


def solution(mesh):
    in_specs = (P(None, None, "grp", "slab"), P(None, None, None, "slab"), P(), P("grp", "slab"))
    out_specs = (P(), P(None, None, None, "slab"), P("grp", "slab"))
    return jax.shard_map(
        per_device, mesh=mesh, in_specs=in_specs, out_specs=out_specs, check_vma=False
    )
```

profile of v0, /device:TPU:0, one launch (start us, length us, event | category | flops | bytes accessed | tf_op | source)
XLA Modules:
  0.0 160.7 jit_solution(7786227598539404116)
XLA Ops:
  7.9 2.2 %fusion.7 = bf16[16,3,2048]{2,1,0:T(4,128)(2,1)S(1)} fusion(pred[2048]{0:T(1024)(128)(4,1)S(1)} %fusion.11, f32[16,3,1,2048]{3,2,1,0:T(1,128)} %param.6), kind=kLoop, calls=%fused_computation.15 | loop fusion | flops 196608 | bytes 591872 | tf_op jit(solution)/shard_map/jit(_where)/select_n | solution.py:39
  10.3 7.4 %fusion = bf16[64,3,2048]{2,1,0:T(4,128)(2,1)S(1)} fusion(pred[2048]{0:T(1024)(128)(4,1)S(1)} %fusion.11, bf16[64,3,4,2048]{3,2,1,0:T(4,128)(2,1)} %param.7, s32[]{:T(128)S(6)} %select_n.42), kind=kLoop, calls=%fused_computation.3 | loop fusion | flops 393216 | bytes 1574916 | tf_op jit(solution)/shard_map/jit(_where)/select_n | solution.py:45
  17.7 0.6 copy.29
  18.4 0.4 fusion.15
  18.8 0.2 copy-done.1
  19.0 42.7 %all-reduce.2 = (f32[80,80]{1,0:T(8,128)S(1)}, f32[]{:T(128)}) all-reduce(f32[80,80]{1,0:T(8,128)S(1)} %fusion.15, f32[]{:T(128)S(6)} %mul.67), channel_id=1, replica_groups=mesh['grp'=4,'slab'=8] {'grp','slab'}, use_global_device_ids=true, to_apply=%region_0.1 | all-reduce | flops 6401 | bytes 51208 | tf_op jit(solution)/shard_map/psum | solution.py:51
  62.4 0.6 multiply_reduce_fusion
  63.7 0.2 fusion.8
  64.1 0.2 fusion.16
  64.6 0.2 fusion.17
  65.0 0.2 fusion.18
  65.4 0.4 convolution_convert_fusion
  65.8 1.2 reshape.69
  67.0 1.5 copy.21
  68.5 41.1 %all-reduce.1 = s32[32]{0:T(128)S(1)} all-reduce(s32[32]{0:T(128)S(1)} %bitcast_dynamic-update-slice_fusion), channel_id=2, replica_groups=mesh['grp'=4,'slab'=8] {'grp','slab'}, use_global_device_ids=true, to_apply=%add.1 | all-reduce | flops 32 | bytes 256
  109.7 37.0 %while.13 = (s32[]{:T(128)}, s32[1,1]{1,0:T(1,128)}, s32[]{:T(128)}, s32[32,1,1]{0,2,1:T(1,128)S(1)}, s32[]{:T(128)}) while((s32[]{:T(128)}, s32[1,1]{1,0:T(1,128)}, s32[]{:T(128)}, s32[32,1,1]{0,2,1:T(1,128)S(1)}, s32[]{:T(128)}) %tuple.42), condition=%wide.region_4.5_spmd, body=%wide.region_3.4_spmd.sunk | while | flops 5 | bytes 115 | solution.py:18
  109.7 0.6 constant_dynamic-slice_fusion.2
  110.8 0.6 constant_dynamic-slice_fusion.2
  112.0 0.6 constant_dynamic-slice_fusion.2
  113.2 0.6 constant_dynamic-slice_fusion.2
  114.4 0.6 constant_dynamic-slice_fusion.2
  115.6 0.6 constant_dynamic-slice_fusion.2
  116.8 0.6 constant_dynamic-slice_fusion.2
  118.0 0.6 constant_dynamic-slice_fusion.2
  119.2 0.6 constant_dynamic-slice_fusion.2
  120.4 0.6 constant_dynamic-slice_fusion.2
  121.6 0.6 constant_dynamic-slice_fusion.2
  122.8 0.6 constant_dynamic-slice_fusion.2
  124.0 0.6 constant_dynamic-slice_fusion.2
  125.2 0.6 constant_dynamic-slice_fusion.2
  126.4 0.6 constant_dynamic-slice_fusion.2
  127.6 0.6 constant_dynamic-slice_fusion.2
  128.8 0.6 constant_dynamic-slice_fusion.2
  130.0 0.6 constant_dynamic-slice_fusion.2
  131.2 0.6 constant_dynamic-slice_fusion.2
  132.4 0.6 constant_dynamic-slice_fusion.2
  133.6 0.6 constant_dynamic-slice_fusion.2
  134.7 0.6 constant_dynamic-slice_fusion.2
  135.9 0.6 constant_dynamic-slice_fusion.2
  137.1 0.6 constant_dynamic-slice_fusion.2
  138.3 0.6 constant_dynamic-slice_fusion.2
  139.5 0.6 constant_dynamic-slice_fusion.2
  140.7 0.6 constant_dynamic-slice_fusion.2
  141.9 0.6 constant_dynamic-slice_fusion.2
  143.1 0.6 constant_dynamic-slice_fusion.2
  144.3 0.6 constant_dynamic-slice_fusion.2
  145.5 0.6 constant_dynamic-slice_fusion.2
  146.7 6.0 %copy.23 = bf16[64,3,4,2048]{3,2,1,0:T(4,128)(2,1)} copy(bf16[64,3,4,2048]{3,0,1,2:T(8,128)(2,1)} %all-gather.3.cloned.1.call-done) | data formatting | bytes 6291456
  (18 shorter events, 1.1 us)
Async XLA Ops:
  7.2 139.5 %all-gather.3.cloned.1.call-start = ((), (), s32[]{:S(2)}) async-start(), calls=%async_computation | async-start | bytes 3932160 | tf_op jit(solution)/shard_map/all_gather | solution.py:57
  18.3 0.7 copy-start.1
  62.4 4.6 %copy-start = (f32[80,80]{1,0:T(8,128)}, f32[80,80]{1,0:T(8,128)S(1)}, u32[]{:S(2)}) copy-start(f32[80,80]{1,0:T(8,128)S(1)} %multiply_divide_fusion) | copy-start | bytes 76804
Sparse Core Ops, SparseCore 0:
  68.6 44.5 all-gather.2
where the time goes:
time: 161 us
  blocking collectives  83.8 us (52%)
  local copies, waits for them, and re-layouts  27.9 us (17%)
  loops' own time  18.8 us (12%)
  between operations  17.3 us (11%)
  other arithmetic  10.3 us (6%)
  matrix products  2.43 us (2%)
    psum x1, blocking collectives, per_device(): summed = lax.psum((partial_terms[0],), ('grp', 'slab'))  42.7 us
    unnamed x1, blocking collectives  41.1 us
    another operation x1, loops' own time, entering(): return lax.fori_loop(0, count - 1, step, total)  18.8 us
    dynamic_slice x31, local copies, waits for them, and re-layouts, step(): longer = join(total, pieces[position])  18.3 us
    select_n x1, other arithmetic, per_device(): jnp.where(own_mask[None, None], own_basis, jnp.zeros((), jnp.bfloat16))  7.39 us
    unnamed x10, local copies, waits for them, and re-layouts  7.03 us
  transfers between devices with their start and end apart: 1, of which 0 were waited for; matrix products, arithmetic and copies ran while one was open for 11% of the time, Pallas kernels for 0%

commit v1 on v0

--- a/solution.py
+++ b/solution.py
@@ -48,7 +48,7 @@
         stacked, stacked, (((1,), (1,)), ((), ())), preferred_element_type=jnp.float32
     )
     partial_terms = (raw_gram,)
-    summed = lax.psum((partial_terms[0],), ("grp", "slab"))
+    summed = lax.psum(lax.psum((partial_terms[0],), "slab"), "grp")
     scales = jnp.concatenate([singular_values, jnp.ones((snap_count,), jnp.float32)])
     gram_matrix = summed[0] * scales[:, None] * scales[None, :] / (3.0 * live_cells)
     mixing = orthonormalize(gram_matrix[:, :rank_count], rank_count)

time: 161 us -> 202 us (1.25)
  blocking collectives: 83.8 us -> 124 us
    psum x1 -> x3, blocking collectives: 42.7 us -> 85.9 us  [the longest x2 43.9 us: per_device(): summed = lax.psum(lax.psum((partial_terms[0],), 'slab'), 'grp')]
    unnamed x1, blocking collectives: 41.1 us -> 37.9 us
  transfers between devices with their start and end apart: 1 -> 1, of which waited for: 0 -> 0; matrix products, arithmetic and copies ran while one was open for 11% -> 9% of each run, Pallas kernels for 0% -> 0%
where the time goes in v1:
time: 202 us; the launch traced here: 200 us
  blocking collectives  124 us (61%)
  local copies, waits for them, and re-layouts  27.7 us (14%)
  loops' own time  18.8 us (9%)
  between operations  17.3 us (9%)
  other arithmetic  10.3 us (5%)
  matrix products  2.45 us (1%)
    psum x2, blocking collectives, per_device(): summed = lax.psum(lax.psum((partial_terms[0],), 'slab'), 'grp')  43.9 us
    psum x1, blocking collectives, per_device(): lax.psum(jnp.sum(thickness).astype(jnp.float32) * PLANE, ('grp', 'slab'))  42 us
    unnamed x1, blocking collectives  37.9 us
    another operation x1, loops' own time, entering(): return lax.fori_loop(0, count - 1, step, total)  18.8 us
    dynamic_slice x31, local copies, waits for them, and re-layouts, step(): longer = join(total, pieces[position])  18.3 us
    select_n x1, other arithmetic, per_device(): jnp.where(own_mask[None, None], own_basis, jnp.zeros((), jnp.bfloat16))  7.39 us
    unnamed x10, local copies, waits for them, and re-layouts  6.82 us
  transfers between devices with their start and end apart: 1, of which 0 were waited for; matrix products, arithmetic and copies ran while one was open for 9% of the time, Pallas kernels for 0%

profile of v1, /device:TPU:0, one launch (start us, length us, event | category | flops | bytes accessed | tf_op | source)
XLA Modules:
  0.0 200.5 jit_solution(3278990580056632643)
XLA Ops:
  7.9 42.0 %psum.23 = f32[]{:T(128)} all-reduce(f32[]{:T(128)S(6)} %mul.67), channel_id=1, replica_groups=mesh['grp'=4,'slab'=8] {'grp','slab'}, use_global_device_ids=true, to_apply=%region_2.3 | all-reduce | flops 1 | bytes 8 | tf_op jit(solution)/shard_map/psum | solution.py:42
  49.9 2.2 %fusion.7 = bf16[16,3,2048]{2,1,0:T(4,128)(2,1)S(1)} fusion(pred[2048]{0:T(1024)(128)(4,1)S(1)} %fusion.11, f32[16,3,1,2048]{3,2,1,0:T(1,128)} %param.6), kind=kLoop, calls=%fused_computation.15 | loop fusion | flops 196608 | bytes 591872 | tf_op jit(solution)/shard_map/jit(_where)/select_n | solution.py:39
  52.3 7.4 %fusion = bf16[64,3,2048]{2,1,0:T(4,128)(2,1)S(1)} fusion(pred[2048]{0:T(1024)(128)(4,1)S(1)} %fusion.11, bf16[64,3,4,2048]{3,2,1,0:T(4,128)(2,1)} %param.7, s32[]{:T(128)S(6)} %select_n.42), kind=kLoop, calls=%fused_computation.3 | loop fusion | flops 393216 | bytes 1574916 | tf_op jit(solution)/shard_map/jit(_where)/select_n | solution.py:45
  59.6 0.6 copy.29
  60.3 0.4 fusion.15
  60.8 27.2 %psum.21 = f32[80,80]{1,0:T(8,128)S(1)} all-reduce(f32[80,80]{1,0:T(8,128)S(1)} %fusion.15), channel_id=1, replica_groups=mesh['grp'=4,'slab'=8] {'slab'}, use_global_device_ids=true, to_apply=%region_0.1 | all-reduce | flops 6400 | bytes 51200 | tf_op jit(solution)/shard_map/psum | solution.py:51
  87.9 16.8 %psum.22 = f32[80,80]{1,0:T(8,128)S(1)} all-reduce(f32[80,80]{1,0:T(8,128)S(1)} %psum.21), channel_id=1, replica_groups=mesh['grp'=4,'slab'=8] {'grp'}, use_global_device_ids=true, to_apply=%region_1.2 | all-reduce | flops 6400 | bytes 51200 | tf_op jit(solution)/shard_map/psum | solution.py:51
  105.5 0.6 multiply_reduce_fusion
  106.8 0.2 fusion.8
  107.2 0.2 fusion.16
  108.0 0.2 fusion.18
  108.5 0.4 convolution_convert_fusion
  108.9 1.2 reshape.69
  110.1 1.5 copy.21
  111.6 37.9 %all-reduce.1 = s32[32]{0:T(128)S(1)} all-reduce(s32[32]{0:T(128)S(1)} %bitcast_dynamic-update-slice_fusion), channel_id=2, replica_groups=mesh['grp'=4,'slab'=8] {'grp','slab'}, use_global_device_ids=true, to_apply=%add.1 | all-reduce | flops 32 | bytes 256
  149.5 37.0 %while.13 = (s32[]{:T(128)}, s32[1,1]{1,0:T(1,128)}, s32[]{:T(128)}, s32[32,1,1]{0,2,1:T(1,128)S(1)}, s32[]{:T(128)}) while((s32[]{:T(128)}, s32[1,1]{1,0:T(1,128)}, s32[]{:T(128)}, s32[32,1,1]{0,2,1:T(1,128)S(1)}, s32[]{:T(128)}) %tuple.42), condition=%wide.region_5.6_spmd, body=%wide.region_4.5_spmd.sunk | while | flops 5 | bytes 115 | solution.py:18
  149.5 0.6 constant_dynamic-slice_fusion.2
  150.7 0.6 constant_dynamic-slice_fusion.2
  151.9 0.6 constant_dynamic-slice_fusion.2
  153.1 0.6 constant_dynamic-slice_fusion.2
  154.2 0.6 constant_dynamic-slice_fusion.2
  155.4 0.6 constant_dynamic-slice_fusion.2
  156.6 0.6 constant_dynamic-slice_fusion.2
  157.8 0.6 constant_dynamic-slice_fusion.2
  159.0 0.6 constant_dynamic-slice_fusion.2
  160.2 0.6 constant_dynamic-slice_fusion.2
  161.4 0.6 constant_dynamic-slice_fusion.2
  162.6 0.6 constant_dynamic-slice_fusion.2
  163.8 0.6 constant_dynamic-slice_fusion.2
  165.0 0.6 constant_dynamic-slice_fusion.2
  166.2 0.6 constant_dynamic-slice_fusion.2
  167.4 0.6 constant_dynamic-slice_fusion.2
  168.6 0.6 constant_dynamic-slice_fusion.2
  169.8 0.6 constant_dynamic-slice_fusion.2
  171.0 0.6 constant_dynamic-slice_fusion.2
  172.2 0.6 constant_dynamic-slice_fusion.2
  173.4 0.6 constant_dynamic-slice_fusion.2
  174.6 0.6 constant_dynamic-slice_fusion.2
  175.8 0.6 constant_dynamic-slice_fusion.2
  177.0 0.6 constant_dynamic-slice_fusion.2
  178.2 0.6 constant_dynamic-slice_fusion.2
  179.3 0.6 constant_dynamic-slice_fusion.2
  180.5 0.6 constant_dynamic-slice_fusion.2
  181.7 0.6 constant_dynamic-slice_fusion.2
  182.9 0.6 constant_dynamic-slice_fusion.2
  184.1 0.6 constant_dynamic-slice_fusion.2
  185.3 0.6 constant_dynamic-slice_fusion.2
  186.5 6.0 %copy.23 = bf16[64,3,4,2048]{3,2,1,0:T(4,128)(2,1)} copy(bf16[64,3,4,2048]{3,0,1,2:T(8,128)(2,1)} %all-gather.3.cloned.1.call-done) | data formatting | bytes 6291456
  (20 shorter events, 1.4 us)
Async XLA Ops:
  7.2 179.4 %all-gather.3.cloned.1.call-start = ((), (), s32[]{:S(2)}) async-start(), calls=%async_computation | async-start | bytes 3932160 | tf_op jit(solution)/shard_map/all_gather | solution.py:57
  60.3 45.0 %copy-start.1 = (f32[64]{0:T(128)S(1)}, f32[64]{0:T(128)}, u32[]{:S(2)}) copy-start(f32[64]{0:T(128)} %param.8) | copy-start | bytes 772
  105.5 4.6 %copy-start = (f32[80,80]{1,0:T(8,128)}, f32[80,80]{1,0:T(8,128)S(1)}, u32[]{:S(2)}) copy-start(f32[80,80]{1,0:T(8,128)S(1)} %multiply_divide_fusion) | copy-start | bytes 76804
Sparse Core Ops, SparseCore 0:
  111.6 41.0 all-gather.2
